TPU v7x, 32 devices: a whole 2x2x4 slice. The times are simulated.
32 devices in a mesh: trial: 2 (over core), bank: 4 (over y, x), zero: 4 (over z).
Axes of the slice: x: 2, y: 2, z: 4, core: 2. Of those that a mesh axis runs over, the one named last changes fastest.
Arguments:
- w_gate: float32 [128, 2048, 1024], P(('trial', 'bank'), 'zero'), parts along dimension 0, may hold values from -0.1875 to 0.1875
- w_up: float32 [128, 2048, 1024], P(('trial', 'bank'), 'zero'), parts along dimension 0, may hold values from -0.1875 to 0.1875
- router_weight: float32 [4096, 64], P(('trial', 'zero'), 'bank'), parts along dimension 0, may hold values from -0.125 to 0.125
- router_gain: float32 [4096], P(('trial', 'zero')), parts along dimension 0, may hold values from 0.25 to 1.75
Outputs:
- serve_gate: bfloat16 [128, 2048, 1024], P(('trial', 'bank'), None, 'zero'), parts along dimension 0
- serve_up: bfloat16 [128, 2048, 1024], P(('trial', 'bank'), None, 'zero'), parts along dimension 0
- scale_gate: float32 [128, 1024], P(('trial', 'bank'), 'zero'), parts along dimension 0
- scale_up: float32 [128, 1024], P(('trial', 'bank'), 'zero'), parts along dimension 0
- serve_router: bfloat16 [4096, 64], P('trial'), parts along dimension 0
There are 2 independent parts, one for each index of `trial`. A program takes and returns all parts, laid end to end along the dimension named above; each array names one. Nothing has to cross between parts.
All inputs are finite; a program needn't handle non-finite values. Where the computation divides by a largest or mean magnitude, that divisor is 1e-20 or more.
Results may differ from a plain program's by a relative error of at most 0.001.
Values may be sent and summed in bfloat16 or wider, within the bound.
A program may use at most 192 MiB of HBM per device.

v0:
```python
import jax
import jax.numpy as jnp
from jax import lax
from jax.sharding import PartitionSpec as P

D_MODEL = 2048


def local(w_gate, w_up, router_weight, router_gain):
    total_gate, total_up = lax.psum(
        (jnp.sum(jnp.abs(w_gate), axis=1), jnp.sum(jnp.abs(w_up), axis=1)), "zero"
    )
    scale_gate = total_gate / D_MODEL
    scale_up = total_up / D_MODEL
    narrow_gate, narrow_up = (
        (w_gate / jnp.expand_dims(scale_gate, 1)).astype(jnp.bfloat16),
        (w_up / jnp.expand_dims(scale_up, 1)).astype(jnp.bfloat16),
    )
    serve_gate, serve_up = (
        lax.all_to_all(narrow_gate, "zero", split_axis=2, concat_axis=1, tiled=True),
        lax.all_to_all(narrow_up, "zero", split_axis=2, concat_axis=1, tiled=True),
    )
    scale_gate = lax.dynamic_slice_in_dim(
        scale_gate, lax.axis_index("zero") * serve_gate.shape[2], serve_gate.shape[2], axis=1
    )
    scale_up = lax.dynamic_slice_in_dim(
        scale_up, lax.axis_index("zero") * serve_up.shape[2], serve_up.shape[2], axis=1
    )
    part_router = (router_weight * router_gain[:, None]).astype(jnp.bfloat16)
    row_router = lax.all_gather(part_router, "zero", axis=0, tiled=True)
    serve_router = lax.all_gather(row_router, "bank", axis=1, tiled=True)
    return (serve_gate, serve_up, scale_gate, scale_up, serve_router)


def solution(mesh):
    placed = (
        P(("trial", "bank"), "zero", None),
        P(("trial", "bank"), "zero", None),
        P(("trial", "zero"), "bank"),
        P(("trial", "zero")),
    )
    return jax.shard_map(
        local,
        mesh=mesh,
        in_specs=placed,
        out_specs=(
            P(("trial", "bank"), None, "zero"),
            P(("trial", "bank"), None, "zero"),
            P(("trial", "bank"), "zero"),
            P(("trial", "bank"), "zero"),
            P("trial", None),
        ),
        check_vma=False,
    )
```

profile of v0, /device:TPU:0, one launch (start us, length us, event | category | flops | bytes accessed | tf_op | source)
XLA Modules:
  0.0 899.1 jit_solution(11479732921372934390)
XLA Ops:
  7.2 0.0 all-reduce.3.cloned.1.call-start
  7.2 22.1 %abs_reduce_fusion = (f32[16,1024]{1,0:T(8,128)}, f32[16,1024]{1,0:T(8,128)}) fusion(f32[16,512,1024]{2,1,0:T(8,128)} %param.5, f32[16,512,1024]{2,1,0:T(8,128)} %param.4), kind=kLoop, calls=%fused_computation.1 | loop fusion | flops 33521664 | bytes 67239936 | tf_op jit(solution)/shard_map/reduce_sum | solution.py:11
  29.3 0.0 all-reduce.3.cloned.1.call-update
  29.3 34.3 %copy.15 = f32[16,512,1024]{1,0,2:T(8,128)} copy(f32[16,512,1024]{2,1,0:T(8,128)} %param.5) | data formatting | bytes 67108864 | tf_op args[1]
  63.6 3.3 all-reduce.3.cloned.1.call-done
  66.9 0.8 broadcast_multiply_fusion
  67.8 0.2 copy.14
  68.0 17.7 %divide_convert_fusion = bf16[16,512,1024]{1,0,2:T(8,128)(2,1)} fusion(f32[16,512,1024]{1,0,2:T(8,128)} %copy.15, f32[16,1024]{0,1:T(8,128)S(1)} %copy.14), kind=kLoop, calls=%fused_computation | loop fusion | flops 16777216 | bytes 50397184 | tf_op jit(solution)/shard_map/convert_element_type | solution.py:17
  85.6 7.1 all-to-all-start.1
  92.7 0.0 copy-start
  92.7 34.2 %copy.12 = f32[16,512,1024]{1,0,2:T(8,128)} copy(f32[16,512,1024]{2,1,0:T(8,128)} %param.4) | data formatting | bytes 67108864 | tf_op args[0]
  126.9 0.0 copy-done
  126.9 0.2 copy.11
  127.1 0.0 copy-start.1
  127.1 0.0 copy-start.2
  127.1 17.7 %divide_convert_fusion.1 = bf16[16,512,1024]{1,0,2:T(8,128)(2,1)} fusion(f32[16,512,1024]{1,0,2:T(8,128)} %copy.12, f32[16,1024]{0,1:T(8,128)S(1)} %copy.11), kind=kLoop, calls=%fused_computation.2 | loop fusion | flops 16777216 | bytes 50397184 | tf_op jit(solution)/shard_map/convert_element_type | solution.py:16
  144.8 308.9 %all-to-all-done.1 = bf16[16,512,1024]{1,0,2:T(8,128)(2,1)} async-done(((bf16[16,512,1024]{1,0,2:T(8,128)(2,1)}), bf16[16,512,1024]{1,0,2:T(8,128)(2,1)}, u32[]{:S(2)}, u32[]{:S(2)}) %all-to-all-start.1) | async-done | bytes 16777248 | tf_op jit(solution)/shard_map/all_to_all | solution.py:21
  453.7 7.0 all-to-all-start
  460.7 0.0 copy-done.1
  460.7 0.0 copy-done.2
  460.8 367.8 %all_gather.6 = bf16[2048,16]{0,1:T(8,128)(2,1)S(1)} all-gather(bf16[512,16]{0,1:T(8,128)(2,1)S(1)} %multiply_convert_fusion), channel_id=1, replica_groups=mesh['trial'=2,'bank'=4,'zero'=4] {'zero'}, dimensions={0}, use_global_device_ids=true | all-gather | bytes 81920 | tf_op jit(solution)/shard_map/all_gather | solution.py:30
  828.5 9.5 %all_gather.7 = bf16[2048,64]{0,1:T(8,128)(2,1)S(1)} all-gather(bf16[2048,16]{0,1:T(8,128)(2,1)S(1)} %all_gather.6), channel_id=1, replica_groups=mesh['trial'=2,'bank'=4,'zero'=4] {'bank'}, dimensions={1}, use_global_device_ids=true | all-gather | bytes 327680 | tf_op jit(solution)/shard_map/all_gather | solution.py:31
  838.0 0.6 constant_dynamic-slice_fusion
  838.6 0.6 constant_dynamic-slice_fusion.1
  839.2 26.2 %copy.16 = bf16[16,4,512,256]{3,2,1,0:T(8,128)(2,1)} copy(bf16[16,4,512,256]{2,0,3,1:T(8,128)(2,1)} %bitcast.4) | data formatting | bytes 33554432 | tf_op jit(solution)/shard_map/all_to_all | solution.py:21
  865.4 0.0 all-to-all-done
  865.4 26.2 %copy.13 = bf16[16,4,512,256]{3,2,1,0:T(8,128)(2,1)} copy(bf16[16,4,512,256]{2,0,3,1:T(8,128)(2,1)} %bitcast.1) | data formatting | bytes 33554432 | tf_op jit(solution)/shard_map/all_to_all | solution.py:20
  891.6 0.7 copy.20
  (2 shorter events, 0.0 us)
Async XLA Ops:
  7.2 59.7 %all-reduce.3.cloned.1.call-start = ((), (), s32[]{:S(2)}) async-start(), calls=%async_computation.2 | async-start | bytes 262144 | tf_op jit(solution)/shard_map/psum | solution.py:10
  85.6 368.1 %all-to-all-start.1 = ((bf16[16,512,1024]{1,0,2:T(8,128)(2,1)}), bf16[16,512,1024]{1,0,2:T(8,128)(2,1)}, u32[]{:S(2)}, u32[]{:S(2)}) async-start(bf16[16,512,1024]{1,0,2:T(8,128)(2,1)} %divide_convert_fusion), calls=%async_computation.1 | async-start | bytes 33554432 | tf_op jit(solution)/shard_map/all_to_all | solution.py:21
  92.7 34.2 %copy-start = (f32[16,1024]{1,0:T(8,128)S(1)}, f32[16,1024]{1,0:T(8,128)}, u32[]{:S(2)}) copy-start(f32[16,1024]{1,0:T(8,128)} %get-tuple-element.5) | copy-start | bytes 196612
  127.1 333.6 %copy-start.1 = (f32[512,16]{0,1:T(8,128)S(1)}, f32[512,16]{0,1:T(8,128)}, u32[]{:S(2)}) copy-start(f32[512,16]{0,1:T(8,128)} %param.6) | copy-start | bytes 98308
  127.1 333.6 %copy-start.2 = (f32[512]{0:T(512)S(1)}, f32[512]{0:T(512)}, u32[]{:S(2)}) copy-start(f32[512]{0:T(512)} %param.7) | copy-start | bytes 6148
  453.7 411.7 %all-to-all-start = ((bf16[16,512,1024]{1,0,2:T(8,128)(2,1)}), bf16[16,512,1024]{1,0,2:T(8,128)(2,1)}, u32[]{:S(2)}, u32[]{:S(2)}) async-start(bf16[16,512,1024]{1,0,2:T(8,128)(2,1)} %divide_convert_fusion.1), calls=%async_computation | async-start | bytes 33554432 | tf_op jit(solution)/shard_map/all_to_all | solution.py:20
Sparse Core Ops, SparseCore 0:
  29.4 37.4 all-reduce.2
where the time goes:
time: 902 us; the launch traced here: 899 us
  blocking collectives  377 us (42%)
  waiting for transfers between devices  312 us (35%)
  local copies, waits for them, and re-layouts  123 us (14%)
  other arithmetic  58.3 us (6%)
  starting transfers between devices  14.1 us (2%)
  between operations  14.1 us (2%)
    all_gather x1, blocking collectives, local(): row_router = lax.all_gather(part_router, 'zero', axis=0, tiled=True)  368 us
    all_to_all x1, waiting for transfers between devices, local(): lax.all_to_all(narrow_up, 'zero', split_axis=2, concat_axis=1, tiled=True)  309 us
    unnamed x9, local copies, waits for them, and re-layouts  69.1 us
    all_to_all x1, local copies, waits for them, and re-layouts, local(): lax.all_to_all(narrow_gate, 'zero', split_axis=2, concat_axis=1, tiled=True)  26.2 us
    all_to_all x1, local copies, waits for them, and re-layouts, local(): lax.all_to_all(narrow_up, 'zero', split_axis=2, concat_axis=1, tiled=True)  26.2 us
    reduce_sum x1, other arithmetic, local(): jnp.sum(jnp.abs(w_up), axis=1)  22.1 us
  transfers between devices with their start and end apart: 3, of which 2 were waited for; matrix products, arithmetic and copies ran while one was open for 13% of the time, Pallas kernels for 0%

commit v1 on v0

--- a/solution.py
+++ b/solution.py
@@ -27,7 +27,8 @@
         scale_up, lax.axis_index("zero") * serve_up.shape[2], serve_up.shape[2], axis=1
     )
     part_router = (router_weight * router_gain[:, None]).astype(jnp.bfloat16)
-    row_router = lax.all_gather(part_router, "zero", axis=0, tiled=True)
+    p_next = lax.all_to_all(jnp.stack([part_router] * lax.psum(1, "zero"), axis=0), "zero", 0, 0)
+    row_router = jnp.concatenate(p_next, axis=0)
     serve_router = lax.all_gather(row_router, "bank", axis=1, tiled=True)
     return (serve_gate, serve_up, scale_gate, scale_up, serve_router)
 

time: 902 us -> 865 us (0.959)
  blocking collectives: 377 us -> 8.98 us
  waiting for transfers between devices: 312 us -> 637 us
    all_gather x1 -> x0, blocking collectives: 368 us -> none  [local(): row_router = lax.all_gather(part_router, 'zero', axis=0, tiled=True)]
    all_to_all x1, waiting for transfers between devices: 0.01 us -> 326 us  [local(): lax.all_to_all(narrow_gate, 'zero', split_axis=2, concat_axis=1, tiled=True)]
  transfers between devices with their start and end apart: 3 -> 4, of which waited for: 2 -> 2; matrix products, arithmetic and copies ran while one was open for 13% -> 15% of each run, Pallas kernels for 0% -> 0%
where the time goes in v1:
time: 865 us; the launch traced here: 862 us
  waiting for transfers between devices  637 us (74%)
  local copies, waits for them, and re-layouts  124 us (14%)
  other arithmetic  58.3 us (7%)
  starting transfers between devices  20.4 us (2%)
  between operations  14.1 us (2%)
  blocking collectives  8.98 us (1%)
    all_to_all x1, waiting for transfers between devices, local(): lax.all_to_all(narrow_gate, 'zero', split_axis=2, concat_axis=1, tiled=True)  326 us
    all_to_all x1, waiting for transfers between devices, local(): lax.all_to_all(narrow_up, 'zero', split_axis=2, concat_axis=1, tiled=True)  311 us
    unnamed x9, local copies, waits for them, and re-layouts  69.1 us
    all_to_all x1, local copies, waits for them, and re-layouts, local(): lax.all_to_all(narrow_gate, 'zero', split_axis=2, concat_axis=1, tiled=True)  26.2 us
    all_to_all x1, local copies, waits for them, and re-layouts, local(): lax.all_to_all(narrow_up, 'zero', split_axis=2, concat_axis=1, tiled=True)  26.2 us
    reduce_sum x1, other arithmetic, local(): jnp.sum(jnp.abs(w_up), axis=1)  22.1 us
    convert_element_type x1, other arithmetic, local(): (w_up / jnp.expand_dims(scale_up, 1)).astype(jnp.bfloat16)  17.7 us
    convert_element_type x1, other arithmetic, local(): (w_gate / jnp.expand_dims(scale_gate, 1)).astype(jnp.bfloat16)  17.7 us
  transfers between devices with their start and end apart: 4, of which 2 were waited for; matrix products, arithmetic and copies ran while one was open for 15% of the time, Pallas kernels for 0%

profile of v1, /device:TPU:0, one launch (start us, length us, event | category | flops | bytes accessed | tf_op | source)
XLA Modules:
  0.0 862.3 jit_solution(10664500630655038486)
XLA Ops:
  7.2 0.0 copy-start.1
  7.2 0.0 copy-start.2
  7.2 0.0 all-reduce.3.cloned.1.call-start
  7.2 22.1 %abs_reduce_fusion = (f32[16,1024]{1,0:T(8,128)}, f32[16,1024]{1,0:T(8,128)}) fusion(f32[16,512,1024]{2,1,0:T(8,128)} %param.5, f32[16,512,1024]{2,1,0:T(8,128)} %param.4), kind=kLoop, calls=%fused_computation.1 | loop fusion | flops 33521664 | bytes 67239936 | tf_op jit(solution)/shard_map/reduce_sum | solution.py:11
  29.3 0.0 all-reduce.3.cloned.1.call-update
  29.3 0.0 copy-done.1
  29.4 0.0 copy-done.2
  29.4 0.6 stack.2
  30.0 6.3 all-to-all-start.2
  36.4 34.3 %copy.21 = f32[16,512,1024]{1,0,2:T(8,128)} copy(f32[16,512,1024]{2,1,0:T(8,128)} %param.5) | data formatting | bytes 67108864 | tf_op args[1]
  70.6 0.0 all-reduce.3.cloned.1.call-done
  70.6 0.8 broadcast_multiply_fusion
  71.5 0.2 copy.20
  71.7 17.7 %divide_convert_fusion = bf16[16,512,1024]{1,0,2:T(8,128)(2,1)} fusion(f32[16,512,1024]{1,0,2:T(8,128)} %copy.21, f32[16,1024]{0,1:T(8,128)S(1)} %copy.20), kind=kLoop, calls=%fused_computation | loop fusion | flops 16777216 | bytes 50397184 | tf_op jit(solution)/shard_map/convert_element_type | solution.py:17
  89.3 0.0 all-to-all-done.2
  89.3 7.1 all-to-all-start.1
  96.4 0.0 copy-start
  96.4 34.1 %copy.18 = f32[16,512,1024]{1,0,2:T(8,128)} copy(f32[16,512,1024]{2,1,0:T(8,128)} %param.4) | data formatting | bytes 67108864 | tf_op args[0]
  130.6 0.0 copy-done
  130.6 0.2 copy.17
  130.8 17.7 %divide_convert_fusion.1 = bf16[16,512,1024]{1,0,2:T(8,128)(2,1)} fusion(f32[16,512,1024]{1,0,2:T(8,128)} %copy.18, f32[16,1024]{0,1:T(8,128)S(1)} %copy.17), kind=kLoop, calls=%fused_computation.2 | loop fusion | flops 16777216 | bytes 50397184 | tf_op jit(solution)/shard_map/convert_element_type | solution.py:16
  148.5 310.7 %all-to-all-done.1 = bf16[16,512,1024]{1,0,2:T(8,128)(2,1)} async-done(((bf16[16,512,1024]{1,0,2:T(8,128)(2,1)}), bf16[16,512,1024]{1,0,2:T(8,128)(2,1)}, u32[]{:S(2)}, u32[]{:S(2)}) %all-to-all-start.1) | async-done | bytes 16777248 | tf_op jit(solution)/shard_map/all_to_all | solution.py:21
  459.2 7.0 all-to-all-start
  466.2 9.0 %all_gather.3 = bf16[2048,64]{0,1:T(8,128)(2,1)S(1)} all-gather(bf16[2048,16]{0,1:T(8,128)(2,1)S(1)} %bitcast.12), channel_id=1, replica_groups=mesh['trial'=2,'bank'=4,'zero'=4] {'bank'}, dimensions={1}, use_global_device_ids=true | all-gather | bytes 327680 | tf_op jit(solution)/shard_map/all_gather | solution.py:32
  475.1 0.6 constant_dynamic-slice_fusion
  475.8 0.6 constant_dynamic-slice_fusion.1
  476.4 26.2 %copy.22 = bf16[16,4,512,256]{3,2,1,0:T(8,128)(2,1)} copy(bf16[16,4,512,256]{2,0,3,1:T(8,128)(2,1)} %bitcast.4) | data formatting | bytes 33554432 | tf_op jit(solution)/shard_map/all_to_all | solution.py:21
  502.5 326.0 %all-to-all-done = bf16[16,512,1024]{1,0,2:T(8,128)(2,1)} async-done(((bf16[16,512,1024]{1,0,2:T(8,128)(2,1)}), bf16[16,512,1024]{1,0,2:T(8,128)(2,1)}, u32[]{:S(2)}, u32[]{:S(2)}) %all-to-all-start) | async-done | bytes 16777248 | tf_op jit(solution)/shard_map/all_to_all | solution.py:20
  828.6 26.2 %copy.19 = bf16[16,4,512,256]{3,2,1,0:T(8,128)(2,1)} copy(bf16[16,4,512,256]{2,0,3,1:T(8,128)(2,1)} %bitcast.1) | data formatting | bytes 33554432 | tf_op jit(solution)/shard_map/all_to_all | solution.py:20
  854.7 0.7 copy.28
  (3 shorter events, 0.0 us)
Async XLA Ops:
  7.2 22.2 %copy-start.1 = (f32[512,16]{0,1:T(8,128)S(1)}, f32[512,16]{0,1:T(8,128)}, u32[]{:S(2)}) copy-start(f32[512,16]{0,1:T(8,128)} %param.6) | copy-start | bytes 98308
  7.2 22.2 %copy-start.2 = (f32[512]{0:T(512)S(1)}, f32[512]{0:T(512)}, u32[]{:S(2)}) copy-start(f32[512]{0:T(512)} %param.7) | copy-start | bytes 6148
  7.2 63.4 %all-reduce.3.cloned.1.call-start = ((), (), s32[]{:S(2)}) async-start(), calls=%async_computation.3 | async-start | bytes 262144 | tf_op jit(solution)/shard_map/psum | solution.py:10
  30.0 59.3 %all-to-all-start.2 = ((bf16[4,512,16]{1,2,0:T(8,128)(2,1)}), bf16[4,512,16]{1,2,0:T(8,128)(2,1)S(1)}, u32[]{:S(2)}, u32[]{:S(2)}) async-start(bf16[4,512,16]{1,2,0:T(8,128)(2,1)} %stack.2), calls=%async_computation.2 | async-start | bytes 131072 | tf_op jit(solution)/shard_map/all_to_all | solution.py:30
  89.3 369.8 %all-to-all-start.1 = ((bf16[16,512,1024]{1,0,2:T(8,128)(2,1)}), bf16[16,512,1024]{1,0,2:T(8,128)(2,1)}, u32[]{:S(2)}, u32[]{:S(2)}) async-start(bf16[16,512,1024]{1,0,2:T(8,128)(2,1)} %divide_convert_fusion), calls=%async_computation.1 | async-start | bytes 33554432 | tf_op jit(solution)/shard_map/all_to_all | solution.py:21
  96.4 34.2 %copy-start = (f32[16,1024]{1,0:T(8,128)S(1)}, f32[16,1024]{1,0:T(8,128)}, u32[]{:S(2)}) copy-start(f32[16,1024]{1,0:T(8,128)} %get-tuple-element.5) | copy-start | bytes 196612
  459.2 369.4 %all-to-all-start = ((bf16[16,512,1024]{1,0,2:T(8,128)(2,1)}), bf16[16,512,1024]{1,0,2:T(8,128)(2,1)}, u32[]{:S(2)}, u32[]{:S(2)}) async-start(bf16[16,512,1024]{1,0,2:T(8,128)(2,1)} %divide_convert_fusion.1), calls=%async_computation | async-start | bytes 33554432 | tf_op jit(solution)/shard_map/all_to_all | solution.py:20
Sparse Core Ops, SparseCore 0:
  29.5 37.5 all-reduce.2
